TPU v7x, 32 devices: a whole 2x2x4 slice. The times are simulated.
32 devices in a mesh: ctx: 8 (over y, x, core), wsh: 4 (over z).
Axes of the slice: x: 2, y: 2, z: 4, core: 2. Of those that a mesh axis runs over, the one named last changes fastest.
Arguments:
- tokens: bfloat16 [4, 1024, 1792], P('wsh', 'ctx'), may hold values from -6 to 6
- cotangent: bfloat16 [4, 1024, 1792], P('wsh', 'ctx'), may hold values from -6 to 6
- segment_ids: int32 [4, 1024], P('wsh'), may hold values from 0 to 23, never falling along the last dimension, each value on 1 to 256 neighbouring positions
- block_order: int32 [16], replicated, may hold values from 0 to 15, as said below
- premix: float32 [1792], P(('ctx', 'wsh')), may hold values from 0.5 to 1.5
- inward: float32 [1792, 2304], P(('ctx', 'wsh')), may hold values from -0.125 to 0.125
- filters: float32 [3, 1792], P(None, ('ctx', 'wsh')), may hold values from -4 to 4
- outward: float32 [1792, 1792], P(('ctx', 'wsh')), may hold values from -1 to 1
- prefeed: float32 [1792], P(('ctx', 'wsh')), may hold values from 0.5 to 1.5
- expand: float32 [1792, 9728], P(('ctx', 'wsh')), may hold values from -0.125 to 0.125
- shrink: float32 [4864, 1792], P(('ctx', 'wsh')), may hold values from -0.078125 to 0.078125
- premix_state: float32 [2, 1792], P(None, ('ctx', 'wsh')), may hold values from -30 to 100, as said below
- inward_state: float32 [2, 1792, 2304], P(None, ('ctx', 'wsh')), may hold values from -30 to 100, as said below
- filters_state: float32 [2, 3, 1792], P(None, None, ('ctx', 'wsh')), may hold values from -30 to 100, as said below
- outward_state: float32 [2, 1792, 1792], P(None, ('ctx', 'wsh')), may hold values from -30 to 100, as said below
- prefeed_state: float32 [2, 1792], P(None, ('ctx', 'wsh')), may hold values from -30 to 100, as said below
- expand_state: float32 [2, 1792, 9728], P(None, ('ctx', 'wsh')), may hold values from -30 to 100, as said below
- shrink_state: float32 [2, 4864, 1792], P(None, ('ctx', 'wsh')), may hold values from -30 to 100, as said below
Outputs:
- block_output: bfloat16 [4, 1024, 1792], P('wsh', 'ctx')
- input_grad: bfloat16 [4, 1024, 1792], P('wsh', 'ctx')
- premix_grad: float32 [1792], P(('ctx', 'wsh'))
- inward_grad: float32 [1792, 2304], P(('ctx', 'wsh'))
- filters_grad: float32 [3, 1792], P(None, ('ctx', 'wsh'))
- outward_grad: float32 [1792, 1792], P(('ctx', 'wsh'))
- prefeed_grad: float32 [1792], P(('ctx', 'wsh'))
- expand_grad: float32 [1792, 9728], P(('ctx', 'wsh'))
- shrink_grad: float32 [4864, 1792], P(('ctx', 'wsh'))
- premix_moments: float32 [2, 1792], P(None, ('ctx', 'wsh'))
- inward_moments: float32 [2, 1792, 2304], P(None, ('ctx', 'wsh'))
- filters_moments: float32 [2, 3, 1792], P(None, None, ('ctx', 'wsh'))
- outward_moments: float32 [2, 1792, 1792], P(None, ('ctx', 'wsh'))
- prefeed_moments: float32 [2, 1792], P(None, ('ctx', 'wsh'))
- expand_moments: float32 [2, 1792, 9728], P(None, ('ctx', 'wsh'))
- shrink_moments: float32 [2, 4864, 1792], P(None, ('ctx', 'wsh'))
- premix_master: float32 [1792], P(('ctx', 'wsh'))
- inward_master: float32 [1792, 2304], P(('ctx', 'wsh'))
- filters_master: float32 [3, 1792], P(None, ('ctx', 'wsh'))
- outward_master: float32 [1792, 1792], P(('ctx', 'wsh'))
- prefeed_master: float32 [1792], P(('ctx', 'wsh'))
- expand_master: float32 [1792, 9728], P(('ctx', 'wsh'))
- shrink_master: float32 [4864, 1792], P(('ctx', 'wsh'))
- weight_norms: float32 [2, 7], replicated
Inputs may be any that keep to these rules, and one draw needn't show every extreme that they name: `segment_ids`: each sequence's segment numbers never fall along positions and start at 0; a segment holds at most 256 positions and one holds exactly that many. `block_order`: A permutation of the 16 blocks; the two slots of each index of ctx hold blocks b and 15 - b for some b. `premix_state`: index 0 holds first moments, index 1 second moments, which are positive. `inward_state`: index 0 holds first moments, index 1 second moments, which are positive. `filters_state`: index 0 holds first moments, index 1 second moments, which are positive. `outward_state`: index 0 holds first moments, index 1 second moments, which are positive. `prefeed_state`: index 0 holds first moments, index 1 second moments, which are positive. `expand_state`: index 0 holds first moments, index 1 second moments, which are positive. `shrink_state`: index 0 holds first moments, index 1 second moments, which are positive.
All inputs are finite; a program needn't handle non-finite values.
Results may differ from a plain program's by a relative error of at most 0.013.
The roundings to bfloat16 on the way count: a program that leaves them out, or rounds other values in their place, can miss the bound.
Values may be sent and summed in bfloat16 or wider, within the bound.
A program may use at most 320 MiB of HBM per device.

v0:
```python
import jax
import jax.numpy as jnp
from jax import lax
from jax.sharding import PartitionSpec as P

HEADS = 16
QUERY_KEY_WIDTH = 16
KCONV = 3
STEP = 3
HDV = 112
QK = 256
TILE = 128
norm_eps = 1e-05
adam_eps = 1e-08
beta_first = 0.9
beta_second = 0.99
learn_rate = 0.5
f32 = jnp.float32
bf16 = jnp.bfloat16
BOTH = ("ctx", "wsh")


def mm(left, right):
    return jnp.dot(left, right, preferred_element_type=f32)


def mm_nt(left, right):
    return lax.dot_general(left, right, (((1,), (1,)), ((), ())), preferred_element_type=f32)


def mm_tn(left, right):
    return lax.dot_general(left, right, (((0,), (0,)), ((), ())), preferred_element_type=f32)


def inverse_rms(values):
    return lax.rsqrt(jnp.mean(values * values, axis=-1, keepdims=True) + norm_eps)


def rms_back(grad_normed, normed, scaler):
    return scaler * (grad_normed - normed * jnp.mean(grad_normed * normed, axis=-1, keepdims=True))


def silu_slope(values):
    sigmoid = jax.nn.sigmoid(values)
    return sigmoid * (1.0 + values * (1.0 - sigmoid))


def gather_rows(values):
    return lax.all_gather(values, "ctx", axis=0, tiled=True)


def scatter_sum(values, ctx):
    rows, columns = values.shape
    pieces = lax.all_to_all(values.reshape(ctx, rows // ctx, columns), "ctx", 0, 0)
    return jnp.sum(pieces.astype(f32), axis=0)


def split_columns(shard, parts, ctx):
    rows = shard.shape[0]
    pieces, start = ([], 0)
    for width in parts:
        piece = shard[:, start : start + width].reshape(rows, ctx, width // ctx)
        pieces.append(piece)
        start += width
    return jnp.transpose(jnp.concatenate(pieces, axis=2), (1, 0, 2))


def join_columns(pieces, parts, ctx):
    moved = jnp.transpose(pieces, (1, 0, 2))
    rows, joined, start = (moved.shape[0], [], 0)
    for width in parts:
        own = width // ctx
        joined.append(moved[:, :, start : start + own].reshape(rows, width))
        start += own
    return jnp.concatenate(joined, axis=1)


def gather_columns(shard, parts, ctx):
    pieces = split_columns(shard, parts, ctx)
    rows, columns = pieces.shape[1:]
    swapped = lax.all_to_all(pieces, "ctx", 0, 0)
    full = lax.all_gather(swapped, "wsh", axis=1)
    return full.reshape(-1, columns)


def return_columns(grad, parts, ctx, wsh):
    columns = grad.shape[1]
    pieces = grad.astype(bf16).reshape(ctx, wsh, -1, columns)
    swapped = lax.all_to_all(pieces, "wsh", 1, 0)
    summed = jnp.sum(swapped.astype(f32), axis=0).astype(bf16)
    back = lax.all_to_all(summed, "ctx", 0, 0)
    return join_columns(back, parts, ctx).astype(f32)


def return_rows(grad, wsh):
    columns = grad.shape[1]
    pieces = grad.astype(bf16).reshape(wsh, -1, columns)
    swapped = lax.all_to_all(pieces, "wsh", 0, 0)
    return jnp.sum(swapped.astype(f32), axis=0)


def windows(values, prior):
    tiles = values.reshape((-1, TILE) + values.shape[1:])
    count = tiles.shape[0]
    padded = jnp.concatenate([jnp.zeros((prior,) + tiles.shape[1:], values.dtype), tiles], axis=0)
    return jnp.concatenate([padded[j : j + count] for j in range(prior + 1)], axis=1)


def unwindow(grads, prior):
    count = grads.shape[0]
    tail = grads.shape[2:]
    pieces = grads.reshape((count, prior + 1, TILE) + tail)
    total = jnp.zeros((count + prior, TILE) + tail, grads.dtype)
    for j in range(prior + 1):
        total = total.at[j : j + count].add(pieces[:, j])
    return total[prior:].reshape((count * TILE,) + tail)


def scores_of(query_tiles, key_windows, allowed):
    scores = jnp.einsum(
        "tqhd,tkhd->htqk", query_tiles, key_windows, preferred_element_type=f32
    ) * QUERY_KEY_WIDTH ** (-0.5)
    return (scores, (1.0 + scores + 0.5 * scores * scores) * allowed[None])


def allowed_of(segments, prior):
    length = segments.shape[0]
    positions = jnp.arange(length, dtype=jnp.int32)
    key_pos = jnp.arange(length, dtype=jnp.int32) + 1
    key_windows = windows(key_pos, prior)
    seg_windows = windows(segments, prior)
    pos_tiles = positions.reshape(-1, TILE)
    seg_tiles = segments.reshape(-1, TILE)
    return (
        (key_windows[:, None, :] >= 1)
        & (key_windows[:, None, :] - 1 <= pos_tiles[:, :, None])
        & (seg_windows[:, None, :] == seg_tiles[:, :, None])
    ).astype(f32)


def shifted(values, offset):
    if offset == 0:
        return values
    rows = values.shape[0]
    edge = jnp.zeros((abs(offset),) + values.shape[1:], values.dtype)
    if offset > 0:
        return jnp.concatenate([edge, values[: rows - offset]], axis=0)
    return jnp.concatenate([values[-offset:], edge], axis=0)


def make_body(ctx, wsh):

    def body(
        tokens,
        cotangent,
        segment_ids,
        block_order,
        premix,
        inward,
        filters,
        outward,
        prefeed,
        expand,
        shrink,
        premix_state,
        inward_state,
        filters_state,
        outward_state,
        prefeed_state,
        expand_state,
        shrink_state,
    ):
        masters = (premix, inward, filters, outward, prefeed, expand, shrink)
        states = (
            premix_state,
            inward_state,
            filters_state,
            outward_state,
            prefeed_state,
            expand_state,
            shrink_state,
        )
        width = tokens.shape[2]
        feed = expand.shape[1] // 2
        segments = segment_ids[0]
        length = segments.shape[0]
        blocks = block_order.shape[0]
        block_rows = length // blocks
        prior = -(-(length // 4 - 1) // TILE)
        heads = HEADS // ctx
        keys_width = QK // ctx
        own_values = width // ctx
        own_feed = feed // ctx
        inverse = (
            jnp.zeros((blocks,), jnp.int32).at[block_order].set(jnp.arange(blocks, dtype=jnp.int32))
        )

        def reorder(values, indices):
            return jnp.take(values.reshape(blocks, block_rows, -1), indices, axis=0).reshape(
                length, -1
            )

        in_parts, ex_parts = ((QK, QK, width), (feed, feed))
        gains = lax.all_gather(
            jnp.stack([premix, prefeed]).astype(bf16), BOTH, axis=1, tiled=True
        ).astype(f32)
        gain_one, gain_two = (gains[0], gains[1])
        taps = lax.all_gather(filters.astype(bf16), "wsh", axis=1, tiled=True).astype(f32)
        inward_own = gather_columns(inward.astype(bf16), in_parts, ctx)
        outward_own = lax.all_gather(outward.astype(bf16), "wsh", axis=0, tiled=True)
        expand_own = gather_columns(expand.astype(bf16), ex_parts, ctx)
        shrink_own = lax.all_gather(shrink.astype(bf16), "wsh", axis=0, tiled=True)
        tokens_all = gather_rows(tokens[0])
        grad_ffn = gather_rows(cotangent[0])
        inputs_all = tokens_all.astype(f32)
        mixed_in = (inputs_all * inverse_rms(inputs_all) * gain_one).astype(bf16)
        project = reorder(mm(mixed_in, inward_own).astype(bf16), inverse)
        queries = project[:, :keys_width].reshape(-1, TILE, heads, QUERY_KEY_WIDTH)
        keys = project[:, keys_width : 2 * keys_width].reshape(length, heads, QUERY_KEY_WIDTH)
        values = project[:, 2 * keys_width :]
        value_float = values.astype(f32)
        usable, tapped = ([], [])
        for offset in range(KCONV):
            usable.append(
                ((shifted(segments, offset) == segments) & (jnp.arange(length) >= offset)).astype(
                    f32
                )[:, None]
            )
            tapped.append(shifted(value_float, offset) * usable[offset])
        convolved = sum((taps[offset] * tapped[offset] for offset in range(KCONV)))
        allowed = allowed_of(segments, prior)
        key_windows = windows(keys, prior)
        value_windows = windows(values.reshape(length, heads, HDV), prior)
        scores, weights = scores_of(queries, key_windows, allowed)
        probs = weights.astype(bf16)
        totals = jnp.sum(weights, axis=3)
        totals_rows = jnp.transpose(totals, (1, 2, 0))[..., None]
        numer = jnp.einsum("htqk,tkhd->tqhd", probs, value_windows, preferred_element_type=f32)
        attended = numer / totals_rows
        attended_flat = attended.reshape(length, own_values)
        conv_gate = jax.nn.silu(convolved)
        gated = reorder((attended_flat * conv_gate).astype(bf16), block_order)
        mixed_out = mm(gated, outward_own).astype(bf16)
        inputs = tokens[0].astype(f32)
        residual = inputs + scatter_sum(mixed_out, ctx)
        scaler_two = inverse_rms(residual)
        normed_two = residual * scaler_two
        feed_in = gather_rows((normed_two * gain_two).astype(bf16))
        gate_up = mm(feed_in, expand_own)
        gate_part, up_part = (gate_up[:, :own_feed], gate_up[:, own_feed:])
        gate_silu = jax.nn.silu(gate_part)
        activated = (gate_silu * up_part).astype(bf16)
        block_output = (residual + scatter_sum(mm(activated, shrink_own).astype(bf16), ctx)).astype(
            bf16
        )
        shrink_grad = mm_tn(activated, grad_ffn)
        grad_act = mm_nt(grad_ffn, shrink_own)
        grad_gate_up = jnp.concatenate(
            [grad_act * up_part * silu_slope(gate_part), grad_act * gate_silu], axis=1
        ).astype(bf16)
        expand_grad = mm_tn(feed_in, grad_gate_up)
        grad_feed = scatter_sum(mm_nt(grad_gate_up, expand_own).astype(bf16), ctx)
        prefeed_part = jnp.sum(grad_feed * normed_two, axis=0)
        grad_resid = cotangent[0].astype(f32) + rms_back(
            grad_feed * gain_two, normed_two, scaler_two
        )
        grad_mix = gather_rows(grad_resid.astype(bf16))
        outward_grad = mm_tn(gated, grad_mix)
        grad_gated = reorder(mm_nt(grad_mix, outward_own), inverse)
        grad_attended = (grad_gated * conv_gate).reshape(-1, TILE, heads, HDV)
        grad_conv = grad_gated * attended_flat * silu_slope(convolved)
        filters_part = jnp.stack(
            [jnp.sum(grad_conv * tapped[offset], axis=0) for offset in range(KCONV)]
        )
        grad_numer = (grad_attended / totals_rows).astype(bf16)
        grad_totals = -jnp.sum(grad_attended * attended, axis=3) / totals_rows[..., 0]
        grad_totals = jnp.transpose(grad_totals, (2, 0, 1))
        grad_weights = (
            jnp.einsum("tqhd,tkhd->htqk", grad_numer, value_windows, preferred_element_type=f32)
            + grad_totals[..., None]
        )
        score_gradient = (grad_weights * (1.0 + scores) * allowed[None]).astype(bf16)
        scale = QUERY_KEY_WIDTH ** (-0.5)
        grad_query = (
            jnp.einsum("htqk,tkhd->tqhd", score_gradient, key_windows, preferred_element_type=f32)
            * scale
        )
        grad_keys = (
            unwindow(
                jnp.einsum("htqk,tqhd->tkhd", score_gradient, queries, preferred_element_type=f32),
                prior,
            )
            * scale
        )
        grad_values = unwindow(
            jnp.einsum("htqk,tqhd->tkhd", probs, grad_numer, preferred_element_type=f32), prior
        ).reshape(length, own_values)
        for offset in range(KCONV):
            grad_values = grad_values + taps[offset] * shifted(grad_conv * usable[offset], -offset)
        grad_project = reorder(
            jnp.concatenate(
                [
                    grad_query.reshape(length, keys_width),
                    grad_keys.reshape(length, keys_width),
                    grad_values,
                ],
                axis=1,
            ).astype(bf16),
            block_order,
        )
        inward_grad = mm_tn(mixed_in, grad_project)
        grad_mixin = scatter_sum(mm_nt(grad_project, inward_own).astype(bf16), ctx)
        scaler_one = inverse_rms(inputs)
        normed_one = inputs * scaler_one
        premix_part = jnp.sum(grad_mixin * normed_one, axis=0)
        input_grad = (grad_resid + rms_back(grad_mixin * gain_one, normed_one, scaler_one)).astype(
            bf16
        )
        gain_grads = lax.psum_scatter(
            jnp.stack([premix_part, prefeed_part]), BOTH, scatter_dimension=1, tiled=True
        )
        shards = (
            gain_grads[0],
            return_columns(inward_grad, in_parts, ctx, wsh),
            lax.psum_scatter(filters_part, "wsh", scatter_dimension=1, tiled=True),
            return_rows(outward_grad, wsh),
            gain_grads[1],
            return_columns(expand_grad, ex_parts, ctx, wsh),
            return_rows(shrink_grad, wsh),
        )
        return (block_output[None], input_grad[None]) + shards + update(masters, states, shards)

    return body


def update(masters, states, shards):
    moments = []
    directions = []
    for state_pair, gradient in zip(states, shards):
        first_moment = beta_first * state_pair[0] + (1.0 - beta_first) * gradient
        second = beta_second * state_pair[1] + (1.0 - beta_second) * gradient * gradient
        directions.append(
            first_moment
            / (1.0 - beta_first**STEP)
            / (jnp.sqrt(second / (1.0 - beta_second**STEP)) + adam_eps)
        )
        moments.append(jnp.stack([first_moment, second]))
    step_sums = jnp.stack([jnp.sum(direction * direction) for direction in directions])
    weight_sums = jnp.stack([jnp.sum(weight * weight) for weight in masters])
    totals = lax.psum(jnp.stack([weight_sums, step_sums]), BOTH)
    norms = jnp.sqrt(totals)
    updated = [
        masters[i] - learn_rate * (norms[0, i] / norms[1, i]) * directions[i] for i in range(7)
    ]
    return tuple(moments) + tuple(updated) + (norms,)


def solution(mesh):
    ctx, wsh = (mesh.shape["ctx"], mesh.shape["wsh"])
    rows, columns, moments_rows = (P(BOTH, None), P(None, BOTH), P(None, BOTH, None))
    vector, whole = (P(BOTH), P("wsh", "ctx", None))
    weights = (vector, rows, columns, rows, vector, rows, rows)
    states = (
        columns,
        moments_rows,
        P(None, None, BOTH),
        moments_rows,
        columns,
        moments_rows,
        moments_rows,
    )
    return jax.shard_map(
        make_body(ctx, wsh),
        mesh=mesh,
        in_specs=(whole, whole, P("wsh", None), P()) + weights + states,
        out_specs=(whole, whole) + weights + states + weights + (P(),),
        check_vma=False,
    )
```

profile of v0, /device:TPU:0, one launch (start us, length us, event | category | flops | bytes accessed | tf_op | source)
XLA Modules:
  0.0 969.0 jit_solution(15023815569160416463)
XLA Ops:
  10.8 5.2 all-to-all-start
  16.7 69.3 %all-gather.4 = bf16[32,56,2]{1,2,0:T(2,128)(2,1)S(1)} all-gather(bf16[1,56,2]{1,2,0:T(2,128)(2,1)S(1)} %maximum_bitcast_fusion.2), channel_id=1, replica_groups=mesh['ctx'=8,'wsh'=4] {'ctx','wsh'}, dimensions={0}, use_global_device_ids=true | all-gather | bytes 7392 | tf_op jit(solution)/shard_map/all_gather | solution.py:204
  86.7 7.6 all-gather.5
  103.6 4.2 all-to-all-start.2
  109.2 18.9 %all_gather.41 = bf16[224,1792]{1,0:T(8,128)(2,1)} all-gather(bf16[56,1792]{1,0:T(8,128)(2,1)S(1)} %get-tuple-element.311), channel_id=1, replica_groups=mesh['ctx'=8,'wsh'=4] {'wsh'}, dimensions={0}, use_global_device_ids=true | all-gather | bytes 1003520 | tf_op jit(solution)/shard_map/all_gather | solution.py:210
  129.0 24.9 %all-gather.1 = bf16[8,224,288]{2,0,1:T(8,128)(2,1)S(1)} all-gather(bf16[8,56,288]{2,0,1:T(8,128)(2,1)S(1)} %copy.320), channel_id=3, replica_groups=mesh['ctx'=8,'wsh'=4] {'wsh'}, dimensions={1}, use_global_device_ids=true | all-gather | bytes 1290240 | tf_op jit(solution)/shard_map/all_gather | solution.py:82
  154.0 2.4 copy.321
  156.4 2.6 reshape.832
  159.4 3.0 fusion
  167.8 3.3 fusion.19
  184.7 47.2 %all_to_all.68 = bf16[8,128,1792]{2,1,0:T(8,128)(2,1)S(1)} all-to-all(bf16[8,128,1792]{2,1,0:T(8,128)(2,1)S(1)} %bitcast.354), channel_id=1, replica_groups=mesh['ctx'=8,'wsh'=4] {'ctx'}, dimensions={0} | all-to-all | bytes 7340032 | tf_op jit(solution)/shard_map/all_to_all | solution.py:54
  237.0 9.8 %all-gather.21.cloned.1.call-done = bf16[8,224,1216]{2,1,0:T(8,128)(2,1)} async-done(((bf16[8,56,1216]{2,1,0:T(8,128)(2,1)}), bf16[8,224,1216]{2,1,0:T(8,128)(2,1)}) %all-gather.21.cloned.1.call-update) | async-done | bytes 4358160 | tf_op jit(solution)/shard_map/all_gather | solution.py:82
  246.8 35.3 %all-gather.13.cloned.1.call-done = bf16[1024,1792]{1,0:T(8,128)(2,1)} async-done(((bf16[128,1792]{1,0:T(8,128)(2,1)}), bf16[1024,1792]{1,0:T(8,128)(2,1)}) %all-gather.13.cloned.1.call-update) | async-done | bytes 3670032 | tf_op jit(solution)/shard_map/all_gather | solution.py:49
  282.1 10.4 %fusion.142 = f32[1024,1216]{0,1:T(8,128)} fusion(bf16[1024,1792]{1,0:T(8,128)(2,1)} %all-gather.13.cloned.1.call-done, bf16[1792,1216]{1,0:T(8,128)(2,1)} %bitcast.412), kind=kOutput, calls=%fused_computation.307 | convolution fusion | flops 4462739456 | bytes 13008896 | tf_op jit(solution)/shard_map/dot_general | solution.py:24
  292.5 38.6 %all-gather.15.cloned.1.call-done = bf16[608,1792]{1,0:T(8,128)(2,1)} async-done(((bf16[152,1792]{1,0:T(8,128)(2,1)}), bf16[608,1792]{1,0:T(8,128)(2,1)}) %all-gather.15.cloned.1.call-update) | async-done | bytes 2179088 | tf_op jit(solution)/shard_map/all_gather | solution.py:212
  331.1 34.9 %all-gather.23.cloned.1.call-done = bf16[1,1024,1792]{2,1,0:T(8,128)(2,1)} async-done(((bf16[1,128,1792]{2,1,0:T(8,128)(2,1)}), bf16[1,1024,1792]{2,1,0:T(8,128)(2,1)}) %all-gather.23.cloned.1.call-update) | async-done | bytes 3670032 | tf_op jit(solution)/shard_map/all_gather | solution.py:49
  366.1 8.4 multiply_convert_fusion.2
  374.4 9.7 convolution_convert_fusion.2
  384.1 4.7 all-to-all-start.4
  388.8 6.9 convolution_convert_fusion.3
  395.8 36.6 %all-to-all-done.4 = bf16[8,128,1792]{2,1,0:T(8,128)(2,1)} async-done(((bf16[8,128,1792]{2,1,0:T(8,128)(2,1)}), bf16[8,128,1792]{2,1,0:T(8,128)(2,1)}, u32[]{:S(2)}, u32[]{:S(2)}) %all-to-all-start.4) | async-done | bytes 3670048 | tf_op jit(solution)/shard_map/all_to_all | solution.py:54
  432.3 4.5 all-to-all-start.3
  436.8 6.2 fusion.7
  443.0 37.3 %all-to-all-done.3 = bf16[8,128,1792]{2,1,0:T(8,128)(2,1)} async-done(((bf16[8,128,1792]{2,1,0:T(8,128)(2,1)}), bf16[8,128,1792]{2,1,0:T(8,128)(2,1)}, u32[]{:S(2)}, u32[]{:S(2)}) %all-to-all-start.3) | async-done | bytes 3670048 | tf_op jit(solution)/shard_map/all_to_all | solution.py:54
  480.3 4.6 all-to-all-start.11
  484.9 9.6 convolution_convert_fusion
  494.5 7.2 copy.370
  501.6 4.7 copy.371
  506.4 25.8 %all-to-all-done.11 = bf16[4,152,1792]{2,1,0:T(8,128)(2,1)} async-done(((bf16[4,152,1792]{2,1,0:T(8,128)(2,1)}), bf16[4,152,1792]{2,1,0:T(8,128)(2,1)}, u32[]{:S(2)}, u32[]{:S(2)}) %all-to-all-start.11) | async-done | bytes 2179104 | tf_op jit(solution)/shard_map/all_to_all | solution.py:98
  532.1 4.9 all-to-all-start.9
  537.3 2.6 convert_reduce_fusion.1
  545.4 5.0 stack.155
  552.1 3.8 convert_reduce_fusion.2
  557.9 80.3 %all-to-all-done.9 = bf16[1,8,4,56,1216]{4,3,1,0,2:T(8,128)(2,1)} async-done(((bf16[1,8,4,56,1216]{4,3,1,0,2:T(8,128)(2,1)}), bf16[1,8,4,56,1216]{4,3,1,0,2:T(8,128)(2,1)}, u32[]{:S(2)}, u32[]{:S(2)}) %all-to-all-start.9) | async-done | bytes 4358176 | tf_op jit(solution)/shard_map/all_to_all | solution.py:89
  638.2 4.4 reduce_sum.346
  642.6 4.9 all-to-all-start.10
  654.2 9.9 %all-to-all-done.10 = bf16[8,56,1216]{2,1,0:T(8,128)(2,1)} async-done(((bf16[8,56,1216]{2,1,0:T(8,128)(2,1)}), bf16[8,56,1216]{2,1,0:T(8,128)(2,1)}, u32[]{:S(2)}, u32[]{:S(2)}) %all-to-all-start.10) | async-done | bytes 1089568 | tf_op jit(solution)/shard_map/all_to_all | solution.py:91
  667.9 2.4 concatenate.156
  670.3 4.4 fusion.143
  674.6 2.9 gather_fusion.1
  677.6 4.4 multiply_reduce_fusion.6
  696.4 3.9 copy.354
  704.7 2.8 reshape.927
  722.0 4.5 convolution_convert_fusion.5
  729.5 4.3 all-to-all-start.6
  733.8 4.5 fusion.11
  738.4 2.4 reshape.859
  740.7 2.4 reshape.858
  743.1 6.9 multiply_reduce_fusion
  751.9 12.1 %all-to-all-done.6 = bf16[1,8,4,56,288]{4,3,1,0,2:T(8,128)(2,1)} async-done(((bf16[1,8,4,56,288]{4,3,1,0,2:T(8,128)(2,1)}), bf16[1,8,4,56,288]{4,3,1,0,2:T(8,128)(2,1)}, u32[]{:S(2)}, u32[]{:S(2)}) %all-to-all-start.6) | async-done | bytes 1032224 | tf_op jit(solution)/shard_map/all_to_all | solution.py:89
  764.0 4.2 all-to-all-start.8
  768.3 4.0 pad_maximum_fusion
  772.3 15.3 %all-reduce.12 = f32[3,224]{1,0:T(4,128)} all-reduce(f32[3,224]{1,0:T(4,128)S(1)} %pad_maximum_fusion.13), channel_id=7, replica_groups=mesh['ctx'=8,'wsh'=4] {'wsh'}, use_global_device_ids=true, to_apply=%region_19.21.clone | all-reduce | flops 672 | bytes 5376
  787.6 2.4 reduce_sum.341
  790.0 5.2 all-to-all-start.7
  795.2 3.9 convolution_convert_fusion.1
  799.2 3.8 all-to-all-done.7
  803.0 4.6 all-to-all-start.5
  818.2 32.9 %all-to-all-done.5 = bf16[8,128,1792]{2,1,0:T(8,128)(2,1)} async-done(((bf16[8,128,1792]{2,1,0:T(8,128)(2,1)}), bf16[8,128,1792]{2,1,0:T(8,128)(2,1)}, u32[]{:S(2)}, u32[]{:S(2)}) %all-to-all-start.5) | async-done | bytes 3670048 | tf_op jit(solution)/shard_map/all_to_all | solution.py:54
  851.1 2.6 convert_reduce_fusion
  854.1 42.1 %all-reduce.11 = f32[2,1792]{1,0:T(2,128)S(1)} all-reduce(f32[2,1792]{1,0:T(2,128)S(1)} %pad_maximum_fusion.12), channel_id=6, replica_groups=mesh['ctx'=8,'wsh'=4] {'ctx','wsh'}, use_global_device_ids=true, to_apply=%region_14.16.clone | all-reduce | flops 3584 | bytes 28672
  897.5 4.6 stack.164
  902.1 39.1 %psum.7 = f32[2,7]{1,0:T(2,128)S(1)} all-reduce(f32[2,7]{1,0:T(2,128)S(1)} %pad_maximum_fusion.17), channel_id=1, replica_groups=mesh['ctx'=8,'wsh'=4] {'ctx','wsh'}, use_global_device_ids=true, to_apply=%region_37.39 | all-reduce | flops 14 | bytes 112 | tf_op jit(solution)/shard_map/psum | solution.py:350
  951.0 3.0 fusion.70
  (389 shorter events, 118.4 us)
Async XLA Ops:
  7.2 152.1 %all-gather.19.cloned.1.call-start = ((), (), s32[]{:S(2)}) async-start(), calls=%async_computation.15 | async-start | bytes 4128768 | tf_op jit(solution)/shard_map/all_gather | solution.py:49
  7.9 8.1 copy-start.93
  7.9 8.1 copy-start.95
  9.3 76.8 %copy-start.70 = (f32[3,56]{1,0:T(4,128)S(1)}, f32[3,56]{1,0:T(4,128)}, u32[]{:S(2)}) copy-start(f32[3,56]{1,0:T(4,128)} %param.38) | copy-start | bytes 2020
  9.3 85.0 %copy-start.8 = (f32[56,9728]{1,0:T(8,128)S(1)}, f32[56,9728]{1,0:T(8,128)}, u32[]{:S(2)}) copy-start(f32[56,9728]{1,0:T(8,128)} %param.41) | copy-start | bytes 6537220
  10.8 92.8 %all-to-all-start = ((bf16[8,56,288]{2,1,0:T(8,128)(2,1)}), bf16[8,56,288]{2,1,0:T(8,128)(2,1)}, u32[]{:S(2)}, u32[]{:S(2)}) async-start(bf16[8,56,288]{2,1,0:T(8,128)(2,1)} %maximum_bitcast_fusion.1), calls=%async_computation | async-start | bytes 688128 | tf_op jit(solution)/shard_map/all_to_all | solution.py:81
  95.6 5.2 copy-start.33
  99.8 440.7 %copy-start.52 = (f32[1792]{0:T(1024)}, f32[1792]{0:T(1024)S(1)}, u32[]{:S(2)}) copy-start(f32[1792]{0:T(1024)S(1)} %get-tuple-element.250) | copy-start | bytes 21508
  99.8 621.4 %copy-start.55 = (f32[1792]{0:T(1024)}, f32[1792]{0:T(1024)S(1)}, u32[]{:S(2)}) copy-start(f32[1792]{0:T(1024)S(1)} %get-tuple-element.249) | copy-start | bytes 21508
  100.3 7.6 copy-start.76
  103.6 55.3 %all-to-all-start.2 = ((bf16[8,56,1216]{2,1,0:T(8,128)(2,1)}), bf16[8,56,1216]{2,1,0:T(8,128)(2,1)}, u32[]{:S(2)}, u32[]{:S(2)}) async-start(bf16[8,56,1216]{2,1,0:T(8,128)(2,1)} %maximum_bitcast_fusion), calls=%async_computation.2 | async-start | bytes 2293760 | tf_op jit(solution)/shard_map/all_to_all | solution.py:81
  107.9 138.9 %all-gather.21.cloned.1.call-start = ((), (), s32[]{:S(2)}) async-start(), calls=%async_computation.16 | async-start | bytes 5734400 | tf_op jit(solution)/shard_map/all_gather | solution.py:82
  109.2 58.7 %copy-start.11 = (f32[8,128,384]{2,1,0:T(8,128)}, f32[8,128,384]{2,1,0:T(8,128)S(1)}, u32[]{:S(2)}) copy-start(f32[8,128,384]{2,1,0:T(8,128)S(1)} %and_convert_fusion) | copy-start | bytes 4718596
  159.0 123.1 %all-gather.13.cloned.1.call-start = ((), (), s32[]{:S(2)}) async-start(), calls=%async_computation.12 | async-start | bytes 4128768 | tf_op jit(solution)/shard_map/all_gather | solution.py:49
  167.3 12.2 %copy-start.4 = (bf16[16,64,288]{2,1,0:T(8,128)(2,1)}, bf16[16,64,288]{2,1,0:T(8,128)(2,1)S(1)}, u32[]{:S(2)}) copy-start(bf16[16,64,288]{2,1,0:T(8,128)(2,1)S(1)} %broadcast_select_fusion.1) | copy-start | bytes 1769476
  234.7 96.4 %all-gather.15.cloned.1.call-start = ((), (), s32[]{:S(2)}) async-start(), calls=%async_computation.13 | async-start | bytes 2723840 | tf_op jit(solution)/shard_map/all_gather | solution.py:212
  236.4 129.7 %all-gather.23.cloned.1.call-start = ((), (), s32[]{:S(2)}) async-start(), calls=%async_computation.17 | async-start | bytes 4128768 | tf_op jit(solution)/shard_map/all_gather | solution.py:49
  374.4 9.7 copy-start.101
  374.4 9.7 copy-start.102
  384.1 48.2 %all-to-all-start.4 = ((bf16[8,128,1792]{2,1,0:T(8,128)(2,1)}), bf16[8,128,1792]{2,1,0:T(8,128)(2,1)}, u32[]{:S(2)}, u32[]{:S(2)}) async-start(bf16[8,128,1792]{2,1,0:T(8,128)(2,1)} %bitcast.366), calls=%async_computation.4 | async-start | bytes 7340032 | tf_op jit(solution)/shard_map/all_to_all | solution.py:54
  432.3 48.0 %all-to-all-start.3 = ((bf16[8,128,1792]{2,1,0:T(8,128)(2,1)}), bf16[8,128,1792]{2,1,0:T(8,128)(2,1)}, u32[]{:S(2)}, u32[]{:S(2)}) async-start(bf16[8,128,1792]{2,1,0:T(8,128)(2,1)} %bitcast.365), calls=%async_computation.3 | async-start | bytes 7340032 | tf_op jit(solution)/shard_map/all_to_all | solution.py:54
  480.3 51.8 %all-to-all-start.11 = ((bf16[4,152,1792]{2,1,0:T(8,128)(2,1)}), bf16[4,152,1792]{2,1,0:T(8,128)(2,1)}, u32[]{:S(2)}, u32[]{:S(2)}) async-start(bf16[4,152,1792]{2,1,0:T(8,128)(2,1)} %bitcast.368), calls=%async_computation.11 | async-start | bytes 4358144 | tf_op jit(solution)/shard_map/all_to_all | solution.py:98
  532.1 106.1 %all-to-all-start.9 = ((bf16[1,8,4,56,1216]{4,3,1,0,2:T(8,128)(2,1)}), bf16[1,8,4,56,1216]{4,3,1,0,2:T(8,128)(2,1)}, u32[]{:S(2)}, u32[]{:S(2)}) async-start(bf16[1,8,4,56,1216]{4,3,1,0,2:T(8,128)(2,1)} %copy.371), calls=%async_computation.9 | async-start | bytes 9175040 | tf_op jit(solution)/shard_map/all_to_all | solution.py:89
  537.1 133.2 %all-gather.17.cloned.1.call-start = ((), (), s32[]{:S(2)}) async-start(), calls=%async_computation.14 | async-start | bytes 4128768 | tf_op jit(solution)/shard_map/all_gather | solution.py:49
  540.4 10.0 %copy-start.89 = (f32[2,3,56]{2,0,1:T(2,128)S(1)}, f32[2,3,56]{2,0,1:T(2,128)}, u32[]{:S(2)}) copy-start(f32[2,3,56]{2,0,1:T(2,128)} %param.45) | copy-start | bytes 4036
  541.3 10.8 %copy-start.90 = (f32[128]{0:T(128)}, f32[128]{0:T(128)S(1)}, u32[]{:S(2)}) copy-start(f32[128]{0:T(128)S(1)} %broadcast_multiply_fusion.1) | copy-start | bytes 1540
  557.9 93.2 %copy-start.5 = (f32[152,1792]{1,0:T(8,128)}, f32[152,1792]{1,0:T(8,128)S(1)}, u32[]{:S(2)}) copy-start(f32[152,1792]{1,0:T(8,128)S(1)} %convert_reduce_fusion.4) | copy-start | bytes 3268612
  642.6 21.5 %all-to-all-start.10 = ((bf16[8,56,1216]{2,1,0:T(8,128)(2,1)}), bf16[8,56,1216]{2,1,0:T(8,128)(2,1)}, u32[]{:S(2)}, u32[]{:S(2)}) async-start(bf16[8,56,1216]{2,1,0:T(8,128)(2,1)} %reduce_sum.346), calls=%async_computation.10 | async-start | bytes 2293760 | tf_op jit(solution)/shard_map/all_to_all | solution.py:91
  665.7 8.9 copy-start.14
  670.3 7.3 copy-start.83
  707.5 10.1 %copy-start.65 = (f32[1,224]{1,0:T(1,128)S(1)}, f32[1,224]{1,0:T(1,128)}, u32[]{:S(2)}) copy-start(f32[1,224]{1,0:T(1,128)} %get-tuple-element.316) | copy-start | bytes 2692
  707.5 10.1 %copy-start.67 = (f32[1,224]{1,0:T(1,128)S(1)}, f32[1,224]{1,0:T(1,128)}, u32[]{:S(2)}) copy-start(f32[1,224]{1,0:T(1,128)} %get-tuple-element.317) | copy-start | bytes 2692
  729.5 34.5 %all-to-all-start.6 = ((bf16[1,8,4,56,288]{4,3,1,0,2:T(8,128)(2,1)}), bf16[1,8,4,56,288]{4,3,1,0,2:T(8,128)(2,1)}, u32[]{:S(2)}, u32[]{:S(2)}) async-start(bf16[1,8,4,56,288]{4,3,1,0,2:T(8,128)(2,1)} %copy.363), calls=%async_computation.6 | async-start | bytes 2752512 | tf_op jit(solution)/shard_map/all_to_all | solution.py:89
  743.1 6.9 copy-start.26
  743.1 6.9 copy-start.99
  764.0 26.0 %all-to-all-start.8 = ((bf16[4,56,1792]{2,1,0:T(8,128)(2,1)}), bf16[4,56,1792]{2,1,0:T(8,128)(2,1)}, u32[]{:S(2)}, u32[]{:S(2)}) async-start(bf16[4,56,1792]{2,1,0:T(8,128)(2,1)} %bitcast.375), calls=%async_computation.8 | async-start | bytes 1605632 | tf_op jit(solution)/shard_map/all_to_all | solution.py:98
  772.3 22.9 %copy-start.39 = (bf16[1792,288]{0,1:T(8,128)(2,1)S(1)}, bf16[1792,288]{0,1:T(8,128)(2,1)}, u32[]{:S(2)}) copy-start(bf16[1792,288]{0,1:T(8,128)(2,1)} %copy-done.38) | copy-start | bytes 3096580
  772.3 22.9 %copy-start.41 = (bf16[16,64,288]{2,1,0:T(8,128)(2,1)S(1)}, bf16[16,64,288]{2,1,0:T(8,128)(2,1)}, u32[]{:S(2)}) copy-start(bf16[16,64,288]{2,1,0:T(8,128)(2,1)} %copy-done.40) | copy-start | bytes 1769476
  790.0 12.9 %all-to-all-start.7 = ((bf16[8,56,288]{2,1,0:T(8,128)(2,1)}), bf16[8,56,288]{2,1,0:T(8,128)(2,1)S(1)}, u32[]{:S(2)}, u32[]{:S(2)}) async-start(bf16[8,56,288]{2,1,0:T(8,128)(2,1)} %reduce_sum.341), calls=%async_computation.7 | async-start | bytes 688128 | tf_op jit(solution)/shard_map/all_to_all | solution.py:91
  803.0 4.7 copy-start.61
  803.0 4.7 copy-start.62
  803.0 4.7 copy-start.63
  803.0 7.8 copy-start.28
  803.0 48.1 %all-to-all-start.5 = ((bf16[8,128,1792]{2,1,0:T(8,128)(2,1)}), bf16[8,128,1792]{2,1,0:T(8,128)(2,1)}, u32[]{:S(2)}, u32[]{:S(2)}) async-start(bf16[8,128,1792]{2,1,0:T(8,128)(2,1)} %bitcast.364), calls=%async_computation.5 | async-start | bytes 7340032 | tf_op jit(solution)/shard_map/all_to_all | solution.py:54
  818.1 35.6 %copy-start.56 = (f32[1792]{0:T(1024)S(1)}, f32[1792]{0:T(1024)}, u32[]{:S(2)}) copy-start(f32[1792]{0:T(1024)} %copy-done.55) | copy-start | bytes 21508
  818.1 35.6 %copy-start.92 = (f32[128]{0:T(128)S(1)}, f32[128]{0:T(128)}, u32[]{:S(2)}) copy-start(f32[128]{0:T(128)} %add_rsqrt_fusion.1) | copy-start | bytes 1540
  818.1 35.9 %copy-start.60 = (f32[1,1792]{1,0:T(1,128)S(1)}, f32[1,1792]{1,0:T(1,128)}, u32[]{:S(2)}) copy-start(f32[1,1792]{1,0:T(1,128)} %stack.133) | copy-start | bytes 21508
  818.1 78.2 %copy-start.87 = (f32[2,56]{1,0:T(2,128)S(1)}, f32[2,56]{1,0:T(2,128)}, u32[]{:S(2)}) copy-start(f32[2,56]{1,0:T(2,128)} %param.47) | copy-start | bytes 1348
  818.2 78.2 %copy-start.88 = (f32[2,56]{1,0:T(2,128)S(1)}, f32[2,56]{1,0:T(2,128)}, u32[]{:S(2)}) copy-start(f32[2,56]{1,0:T(2,128)} %param.43) | copy-start | bytes 1348
  818.2 83.9 %copy-start.97 = (f32[7]{0:T(128)S(1)}, f32[7]{0:T(128)}, u32[]{:S(2)}) copy-start(f32[7]{0:T(128)} %stack.155) | copy-start | bytes 88
  818.2 132.7 %copy-start.2 = (f32[128,1792]{1,0:T(8,128)S(1)}, f32[128,1792]{1,0:T(8,128)}, u32[]{:S(2)}) copy-start(f32[128,1792]{1,0:T(8,128)} %copy-done.1) | copy-start | bytes 2752516
  818.2 132.7 %copy-start.53 = (f32[1792]{0:T(1024)S(1)}, f32[1792]{0:T(1024)}, u32[]{:S(2)}) copy-start(f32[1792]{0:T(1024)} %copy-done.52) | copy-start | bytes 21508
  818.2 132.7 %copy-start.75 = (f32[128]{0:T(128)S(1)}, f32[128]{0:T(128)}, u32[]{:S(2)}) copy-start(f32[128]{0:T(128)} %copy-done.73) | copy-start | bytes 1540
  818.2 132.7 %copy-start.91 = (f32[128]{0:T(128)S(1)}, f32[128]{0:T(128)}, u32[]{:S(2)}) copy-start(f32[128]{0:T(128)} %copy-done.90) | copy-start | bytes 1540
  941.2 12.8 %copy-start.57 = (f32[2,7]{1,0:T(2,128)}, f32[2,7]{1,0:T(2,128)S(1)}, u32[]{:S(2)}) copy-start(f32[2,7]{1,0:T(2,128)S(1)} %sqrt.31) | copy-start | bytes 172
  950.9 4.3 copy-start.94
  950.9 4.8 copy-start.16
  950.9 4.8 copy-start.30
  950.9 5.6 copy-start.69
  950.9 5.6 copy-start.71
  950.9 6.2 copy-start.34
  950.9 6.2 copy-start.35
  951.0 7.5 copy-start.10
  954.0 4.4 copy-start.9
  (56 other events, 143.9 us)
Sparse Core Ops, SparseCore 0:
  9.9 37.5 all-gather.18
  159.1 87.6 all-gather.20
  249.2 32.8 all-gather.12
  284.1 46.9 all-gather.14
  332.8 33.1 all-gather.22
  542.6 36.9 all-gather.16
where the time goes:
time: 977 us; the launch traced here: 969 us
  waiting for transfers between devices  358 us (37%)
  blocking collectives  264 us (27%)
  local copies, waits for them, and re-layouts  96.8 us (10%)
  other arithmetic  90.9 us (9%)
  matrix products  80.6 us (8%)
  starting transfers between devices  52.7 us (5%)
  between operations  25.6 us (3%)
    all_to_all x3, waiting for transfers between devices, scatter_sum(): lax.all_to_all(values.reshape(ctx, rows // ctx, columns), 'ctx', 0, 0)  107 us
    all_to_all x2, waiting for transfers between devices, return_columns(): swapped = lax.all_to_all(pieces, 'wsh', 1, 0)  92.5 us
    all_gather x4, waiting for transfers between devices, gather_rows(): return lax.all_gather(values, 'ctx', axis=0, tiled=True)  70.3 us
    all_gather x1, blocking collectives, body(): lax.all_gather(jnp.stack([premix, prefeed]).astype(bf16), BOTH, axis=1, t...  69.3 us
    unnamed x2, blocking collectives  57.4 us
    all_to_all x1, blocking collectives, scatter_sum(): lax.all_to_all(values.reshape(ctx, rows // ctx, columns), 'ctx', 0, 0)  47.2 us
    psum x1, blocking collectives, update(): totals = lax.psum(jnp.stack([weight_sums, step_sums]), BOTH)  39.1 us
    all_gather x1, waiting for transfers between devices, body(): shrink_own = lax.all_gather(shrink.astype(bf16), 'wsh', axis=0, tiled=True)  38.6 us
  transfers between devices with their start and end apart: 17, of which 12 were waited for; matrix products, arithmetic and copies ran while one was open for 17% of the time, Pallas kernels for 0%

commit v1 on v0

--- a/solution.py
+++ b/solution.py
@@ -18,6 +18,24 @@
 f32 = jnp.float32
 bf16 = jnp.bfloat16
 BOTH = ("ctx", "wsh")
+
+
+def view_points(x_in, axis_key):
+    r2 = lax.axis_size(axis_key)
+    y, big, near = (r2, lax.axis_index(axis_key), x_in.shape[1])
+    tile_out, r1 = (x_in, 1)
+    while r1 < y:
+        tile_out = jnp.concatenate(
+            [
+                tile_out,
+                lax.ppermute(
+                    tile_out, axis_key, perm=list(map(lambda no: (no, (no - r1) % y), range(y)))
+                ),
+            ],
+            axis=1,
+        )
+        r1 = 2 * r1
+    return jnp.roll(tile_out, big * near, axis=1)
 
 
 def mm(left, right):
@@ -201,9 +219,7 @@
             )
 
         in_parts, ex_parts = ((QK, QK, width), (feed, feed))
-        gains = lax.all_gather(
-            jnp.stack([premix, prefeed]).astype(bf16), BOTH, axis=1, tiled=True
-        ).astype(f32)
+        gains = view_points(jnp.stack([premix, prefeed]).astype(bf16), axis_key=BOTH).astype(f32)
         gain_one, gain_two = (gains[0], gains[1])
         taps = lax.all_gather(filters.astype(bf16), "wsh", axis=1, tiled=True).astype(f32)
         inward_own = gather_columns(inward.astype(bf16), in_parts, ctx)

time: 977 us -> 939 us (0.961)
  blocking collectives: 264 us -> 194 us
  waiting for transfers between devices: 358 us -> 373 us
  starting transfers between devices: 52.7 us -> 63.1 us
    all_gather x1 -> x0, blocking collectives: 69.3 us -> none  [body(): lax.all_gather(jnp.stack([premix, prefeed]).astype(bf16), BOTH, axis=1, t...]
    ppermute x0 -> x5, waiting for transfers between devices: none -> 16 us  [view_points(): lax.ppermute(tile_out, axis_key, perm=list(map(lambda no: (no, (no - r1)...]
    ppermute x0 -> x5, starting transfers between devices: none -> 10.3 us  [view_points(): lax.ppermute(tile_out, axis_key, perm=list(map(lambda no: (no, (no - r1)...]
  transfers between devices with their start and end apart: 17 -> 22, of which waited for: 12 -> 15; matrix products, arithmetic and copies ran while one was open for 17% -> 19% of each run, Pallas kernels for 0% -> 0%
where the time goes in v1:
time: 939 us; the launch traced here: 930 us
  waiting for transfers between devices  373 us (40%)
  blocking collectives  194 us (21%)
  local copies, waits for them, and re-layouts  99.9 us (11%)
  other arithmetic  93.8 us (10%)
  matrix products  80.6 us (9%)
  starting transfers between devices  63.1 us (7%)
  between operations  25.9 us (3%)
    all_to_all x3, waiting for transfers between devices, scatter_sum(): lax.all_to_all(values.reshape(ctx, rows // ctx, columns), 'ctx', 0, 0)  107 us
    all_to_all x2, waiting for transfers between devices, return_columns(): swapped = lax.all_to_all(pieces, 'wsh', 1, 0)  92.3 us
    all_gather x4, waiting for transfers between devices, gather_rows(): return lax.all_gather(values, 'ctx', axis=0, tiled=True)  70.3 us
    unnamed x2, blocking collectives  57.4 us
    all_to_all x1, blocking collectives, scatter_sum(): lax.all_to_all(values.reshape(ctx, rows // ctx, columns), 'ctx', 0, 0)  45.9 us
    psum x1, blocking collectives, update(): totals = lax.psum(jnp.stack([weight_sums, step_sums]), BOTH)  39.1 us
    all_gather x1, waiting for transfers between devices, body(): shrink_own = lax.all_gather(shrink.astype(bf16), 'wsh', axis=0, tiled=True)  38.6 us
    dot_general x4, matrix products, mm_nt(): lax.dot_general(left, right, (((1,), (1,)), ((), ())), preferred_element_...  26.4 us
  transfers between devices with their start and end apart: 22, of which 15 were waited for; matrix products, arithmetic and copies ran while one was open for 19% of the time, Pallas kernels for 0%

profile of v1, /device:TPU:0, one launch (start us, length us, event | category | flops | bytes accessed | tf_op | source)
XLA Modules:
  0.0 930.2 jit_solution(15100158912243776062)
XLA Ops:
  12.4 5.2 all-to-all-start
  18.8 6.0 collective-permute-start
  25.3 7.6 all-gather.4
  40.6 18.3 %all_gather.37 = bf16[224,1792]{1,0:T(8,128)(2,1)} all-gather(bf16[56,1792]{1,0:T(8,128)(2,1)S(1)} %get-tuple-element.311), channel_id=1, replica_groups=mesh['ctx'=8,'wsh'=4] {'wsh'}, dimensions={0}, use_global_device_ids=true | all-gather | bytes 1003520 | tf_op jit(solution)/shard_map/all_gather | solution.py:226
  60.9 3.9 collective-permute-done.1
  65.6 4.3 all-to-all-start.2
  70.6 2.8 collective-permute-start.3
  74.0 11.3 %collective-permute-done.3 = bf16[2,448]{1,0:T(2,128)(2,1)S(1)} collective-permute-done((bf16[2,448]{1,0:T(2,128)(2,1)S(1)}, bf16[2,448]{1,0:T(2,128)(2,1)S(1)}, u32[]{:S(2)}, u32[]{:S(2)}) %collective-permute-start.3) | collective-permute-done | bytes 1824 | tf_op jit(solution)/shard_map/ppermute | solution.py:31
  91.8 25.3 %all-gather.1 = bf16[8,224,288]{2,0,1:T(8,128)(2,1)S(1)} all-gather(bf16[8,56,288]{2,0,1:T(8,128)(2,1)S(1)} %copy.315), channel_id=3, replica_groups=mesh['ctx'=8,'wsh'=4] {'wsh'}, dimensions={1}, use_global_device_ids=true | all-gather | bytes 1290240 | tf_op jit(solution)/shard_map/all_gather | solution.py:100
  117.1 2.4 copy.316
  119.5 2.6 reshape.832
  122.6 3.0 fusion
  131.0 3.3 fusion.19
  148.0 45.9 %all_to_all.68 = bf16[8,128,1792]{2,1,0:T(8,128)(2,1)S(1)} all-to-all(bf16[8,128,1792]{2,1,0:T(8,128)(2,1)S(1)} %bitcast.347), channel_id=1, replica_groups=mesh['ctx'=8,'wsh'=4] {'ctx'}, dimensions={0} | all-to-all | bytes 7340032 | tf_op jit(solution)/shard_map/all_to_all | solution.py:72
  198.9 8.9 all-gather.20.cloned.1.call-done
  207.8 35.3 %all-gather.12.cloned.1.call-done = bf16[1024,1792]{1,0:T(8,128)(2,1)} async-done(((bf16[128,1792]{1,0:T(8,128)(2,1)}), bf16[1024,1792]{1,0:T(8,128)(2,1)}) %all-gather.12.cloned.1.call-update) | async-done | bytes 3670032 | tf_op jit(solution)/shard_map/all_gather | solution.py:67
  243.1 10.4 %fusion.142 = f32[1024,1216]{0,1:T(8,128)} fusion(bf16[1024,1792]{1,0:T(8,128)(2,1)} %all-gather.12.cloned.1.call-done, bf16[1792,1216]{1,0:T(8,128)(2,1)} %bitcast.404), kind=kOutput, calls=%fused_computation.310 | convolution fusion | flops 4462739456 | bytes 13008896 | tf_op jit(solution)/shard_map/dot_general | solution.py:42
  253.5 38.6 %all-gather.14.cloned.1.call-done = bf16[608,1792]{1,0:T(8,128)(2,1)} async-done(((bf16[152,1792]{1,0:T(8,128)(2,1)}), bf16[608,1792]{1,0:T(8,128)(2,1)}) %all-gather.14.cloned.1.call-update) | async-done | bytes 2179088 | tf_op jit(solution)/shard_map/all_gather | solution.py:228
  292.1 34.9 %all-gather.22.cloned.1.call-done = bf16[1,1024,1792]{2,1,0:T(8,128)(2,1)} async-done(((bf16[1,128,1792]{2,1,0:T(8,128)(2,1)}), bf16[1,1024,1792]{2,1,0:T(8,128)(2,1)}) %all-gather.22.cloned.1.call-update) | async-done | bytes 3670032 | tf_op jit(solution)/shard_map/all_gather | solution.py:67
  327.1 8.4 multiply_convert_fusion.2
  335.4 9.7 %convolution_convert_fusion.2 = bf16[1024,1792]{1,0:T(8,128)(2,1)} fusion(bf16[1792,1216]{1,0:T(8,128)(2,1)} %bitcast.405, bf16[1024,608]{0,1:T(8,128)(2,1)S(1)} %get-tuple-element.274, bf16[1024,608]{0,1:T(8,128)(2,1)S(1)} %get-tuple-element.273), kind=kOutput, calls=%fused_computation.18 | convolution fusion | flops 4469555200 | bytes 10518528 | tf_op jit(solution)/shard_map/dot_general | solution.py:46
  345.1 4.7 all-to-all-start.4
  349.9 6.9 convolution_convert_fusion.3
  356.8 36.6 %all-to-all-done.4 = bf16[8,128,1792]{2,1,0:T(8,128)(2,1)} async-done(((bf16[8,128,1792]{2,1,0:T(8,128)(2,1)}), bf16[8,128,1792]{2,1,0:T(8,128)(2,1)}, u32[]{:S(2)}, u32[]{:S(2)}) %all-to-all-start.4) | async-done | bytes 3670048 | tf_op jit(solution)/shard_map/all_to_all | solution.py:72
  393.3 4.5 all-to-all-start.3
  397.8 6.2 fusion.7
  404.0 37.3 %all-to-all-done.3 = bf16[8,128,1792]{2,1,0:T(8,128)(2,1)} async-done(((bf16[8,128,1792]{2,1,0:T(8,128)(2,1)}), bf16[8,128,1792]{2,1,0:T(8,128)(2,1)}, u32[]{:S(2)}, u32[]{:S(2)}) %all-to-all-start.3) | async-done | bytes 3670048 | tf_op jit(solution)/shard_map/all_to_all | solution.py:72
  441.3 4.6 all-to-all-start.11
  445.9 9.6 %convolution_convert_fusion = bf16[1792,1216]{0,1:T(8,128)(2,1)} fusion(bf16[1024,1792]{1,0:T(8,128)(2,1)} %all-gather.12.cloned.1.call-done, bf16[1024,608]{0,1:T(8,128)(2,1)} %copy-done.106, bf16[1024,608]{0,1:T(8,128)(2,1)} %copy-done.105), kind=kOutput, calls=%fused_computation.7 | convolution fusion | flops 4469899264 | bytes 10518528 | tf_op jit(solution)/shard_map/dot_general | solution.py:50
  455.5 7.2 copy.365
  462.7 4.8 copy.366
  467.5 25.6 %all-to-all-done.11 = bf16[4,152,1792]{2,1,0:T(8,128)(2,1)} async-done(((bf16[4,152,1792]{2,1,0:T(8,128)(2,1)}), bf16[4,152,1792]{2,1,0:T(8,128)(2,1)}, u32[]{:S(2)}, u32[]{:S(2)}) %all-to-all-start.11) | async-done | bytes 2179104 | tf_op jit(solution)/shard_map/all_to_all | solution.py:116
  493.2 4.9 all-to-all-start.9
  498.5 2.6 convert_reduce_fusion.1
  506.6 5.1 stack.155
  513.4 3.8 convert_reduce_fusion.2
  519.2 80.1 %all-to-all-done.9 = bf16[1,8,4,56,1216]{4,3,1,0,2:T(8,128)(2,1)} async-done(((bf16[1,8,4,56,1216]{4,3,1,0,2:T(8,128)(2,1)}), bf16[1,8,4,56,1216]{4,3,1,0,2:T(8,128)(2,1)}, u32[]{:S(2)}, u32[]{:S(2)}) %all-to-all-start.9) | async-done | bytes 4358176 | tf_op jit(solution)/shard_map/all_to_all | solution.py:107
  599.3 4.4 reduce_sum.346
  603.6 4.9 all-to-all-start.10
  615.2 9.9 %all-to-all-done.10 = bf16[8,56,1216]{2,1,0:T(8,128)(2,1)} async-done(((bf16[8,56,1216]{2,1,0:T(8,128)(2,1)}), bf16[8,56,1216]{2,1,0:T(8,128)(2,1)}, u32[]{:S(2)}, u32[]{:S(2)}) %all-to-all-start.10) | async-done | bytes 1089568 | tf_op jit(solution)/shard_map/all_to_all | solution.py:109
  631.3 4.4 fusion.143
  635.7 2.9 gather_fusion.1
  638.6 4.4 multiply_reduce_fusion.6
  657.5 3.6 copy.349
  665.5 2.8 reshape.924
  682.9 4.5 convolution_convert_fusion.5
  690.4 4.3 all-to-all-start.6
  694.7 4.5 fusion.11
  701.5 2.4 reshape.858
  703.9 6.9 multiply_reduce_fusion
  712.7 12.2 %all-to-all-done.6 = bf16[1,8,4,56,288]{4,3,1,0,2:T(8,128)(2,1)} async-done(((bf16[1,8,4,56,288]{4,3,1,0,2:T(8,128)(2,1)}), bf16[1,8,4,56,288]{4,3,1,0,2:T(8,128)(2,1)}, u32[]{:S(2)}, u32[]{:S(2)}) %all-to-all-start.6) | async-done | bytes 1032224 | tf_op jit(solution)/shard_map/all_to_all | solution.py:107
  724.9 4.2 all-to-all-start.8
  729.2 4.0 pad_maximum_fusion
  733.2 15.3 %all-reduce.12 = f32[3,224]{1,0:T(4,128)} all-reduce(f32[3,224]{1,0:T(4,128)S(1)} %pad_maximum_fusion.13), channel_id=7, replica_groups=mesh['ctx'=8,'wsh'=4] {'wsh'}, use_global_device_ids=true, to_apply=%region_19.21.clone | all-reduce | flops 672 | bytes 5376
  750.9 5.2 all-to-all-start.7
  756.1 3.9 convolution_convert_fusion.1
  760.1 3.8 all-to-all-done.7
  763.9 4.7 all-to-all-start.5
  779.2 32.9 %all-to-all-done.5 = bf16[8,128,1792]{2,1,0:T(8,128)(2,1)} async-done(((bf16[8,128,1792]{2,1,0:T(8,128)(2,1)}), bf16[8,128,1792]{2,1,0:T(8,128)(2,1)}, u32[]{:S(2)}, u32[]{:S(2)}) %all-to-all-start.5) | async-done | bytes 3670048 | tf_op jit(solution)/shard_map/all_to_all | solution.py:72
  812.0 2.6 convert_reduce_fusion
  815.1 42.1 %all-reduce.11 = f32[2,1792]{1,0:T(2,128)S(1)} all-reduce(f32[2,1792]{1,0:T(2,128)S(1)} %pad_maximum_fusion.12), channel_id=6, replica_groups=mesh['ctx'=8,'wsh'=4] {'ctx','wsh'}, use_global_device_ids=true, to_apply=%region_14.16.clone | all-reduce | flops 3584 | bytes 28672
  858.4 4.6 stack.164
  863.0 39.1 %psum.7 = f32[2,7]{1,0:T(2,128)S(1)} all-reduce(f32[2,7]{1,0:T(2,128)S(1)} %pad_maximum_fusion.19), channel_id=1, replica_groups=mesh['ctx'=8,'wsh'=4] {'ctx','wsh'}, use_global_device_ids=true, to_apply=%region_37.39 | all-reduce | flops 14 | bytes 112 | tf_op jit(solution)/shard_map/psum | solution.py:366
  912.1 3.0 fusion.70
  (410 shorter events, 134.4 us)
Async XLA Ops:
  7.2 115.4 %all-gather.18.cloned.1.call-start = ((), (), s32[]{:S(2)}) async-start(), calls=%async_computation.15 | async-start | bytes 4128768 | tf_op jit(solution)/shard_map/all_gather | solution.py:67
  7.9 9.7 %copy-start.97 = (f32[56]{0:T(128)S(1)}, f32[56]{0:T(128)}, u32[]{:S(2)}) copy-start(f32[56]{0:T(128)} %param.36) | copy-start | bytes 676
  7.9 9.7 %copy-start.99 = (f32[56]{0:T(128)S(1)}, f32[56]{0:T(128)}, u32[]{:S(2)}) copy-start(f32[56]{0:T(128)} %param.40) | copy-start | bytes 676
  7.9 16.8 %copy-start.70 = (f32[3,56]{1,0:T(4,128)S(1)}, f32[3,56]{1,0:T(4,128)}, u32[]{:S(2)}) copy-start(f32[3,56]{1,0:T(4,128)} %param.38) | copy-start | bytes 2020
  8.0 25.0 %copy-start.8 = (f32[56,9728]{1,0:T(8,128)S(1)}, f32[56,9728]{1,0:T(8,128)}, u32[]{:S(2)}) copy-start(f32[56,9728]{1,0:T(8,128)} %param.41) | copy-start | bytes 6537220
  12.4 53.1 %all-to-all-start = ((bf16[8,56,288]{2,1,0:T(8,128)(2,1)}), bf16[8,56,288]{2,1,0:T(8,128)(2,1)}, u32[]{:S(2)}, u32[]{:S(2)}) async-start(bf16[8,56,288]{2,1,0:T(8,128)(2,1)} %maximum_bitcast_fusion.1), calls=%async_computation | async-start | bytes 688128 | tf_op jit(solution)/shard_map/all_to_all | solution.py:99
  18.2 16.1 %copy-start.73 = (bf16[1,56]{1,0:T(2,128)(2,1)}, bf16[1,56]{1,0:T(2,128)(2,1)S(1)}, u32[]{:S(2)}) copy-start(bf16[1,56]{1,0:T(2,128)(2,1)S(1)} %get-tuple-element.355) | copy-start | bytes 340
  18.2 16.1 %copy-start.75 = (bf16[1,56]{1,0:T(2,128)(2,1)}, bf16[1,56]{1,0:T(2,128)(2,1)S(1)}, u32[]{:S(2)}) copy-start(bf16[1,56]{1,0:T(2,128)(2,1)S(1)} %get-tuple-element.359) | copy-start | bytes 340
  18.8 40.8 %collective-permute-start = (bf16[2,56]{1,0:T(2,128)(2,1)}, bf16[2,56]{1,0:T(2,128)(2,1)}, u32[]{:S(2)}, u32[]{:S(2)}) collective-permute-start(bf16[2,56]{1,0:T(2,128)(2,1)} %pad_maximum_fusion.20), channel_id=1, source_target_pairs={{0,31},{1,0},{2,1},{3,2},{4,3},{5,4},{6,5},{7,6},{8,7},{9,8},{10,9... | collective-permute-start | bytes 680 | tf_op jit(solution)/shard_map/ppermute | solution.py:31
  38.6 20.3 %copy-start.102 = (s32[16]{0:T(128)S(1)}, s32[16]{0:T(128)}, u32[]{:S(2)}) copy-start(s32[16]{0:T(128)} %param.35) | copy-start | bytes 196
  38.6 21.0 %copy-start.74 = (bf16[1,56]{1,0:T(2,128)(2,1)S(1)}, bf16[1,56]{1,0:T(2,128)(2,1)}, u32[]{:S(2)}) copy-start(bf16[1,56]{1,0:T(2,128)(2,1)} %copy-done.73) | copy-start | bytes 340
  38.6 21.0 %copy-start.76 = (bf16[1,56]{1,0:T(2,128)(2,1)S(1)}, bf16[1,56]{1,0:T(2,128)(2,1)}, u32[]{:S(2)}) copy-start(bf16[1,56]{1,0:T(2,128)(2,1)} %copy-done.75) | copy-start | bytes 340
  39.1 92.0 %copy-start.11 = (f32[8,128,384]{2,1,0:T(8,128)}, f32[8,128,384]{2,1,0:T(8,128)S(1)}, u32[]{:S(2)}) copy-start(f32[8,128,384]{2,1,0:T(8,128)S(1)} %and_convert_fusion) | copy-start | bytes 4718596
  60.3 4.5 collective-permute-start.1
  60.9 29.9 %copy-start.80 = (pred[16]{0:T(512)(128)(4,1)}, pred[16]{0:T(512)(128)(4,1)S(1)}, u32[]{:S(2)}) copy-start(pred[16]{0:T(512)(128)(4,1)S(1)} %get-tuple-element.362) | copy-start | bytes 52
  65.5 4.3 collective-permute-start.2
  65.6 56.5 %all-to-all-start.2 = ((bf16[8,56,1216]{2,1,0:T(8,128)(2,1)}), bf16[8,56,1216]{2,1,0:T(8,128)(2,1)}, u32[]{:S(2)}, u32[]{:S(2)}) async-start(bf16[8,56,1216]{2,1,0:T(8,128)(2,1)} %maximum_bitcast_fusion), calls=%async_computation.2 | async-start | bytes 2293760 | tf_op jit(solution)/shard_map/all_to_all | solution.py:99
  69.8 137.9 %all-gather.20.cloned.1.call-start = ((), (), s32[]{:S(2)}) async-start(), calls=%async_computation.16 | async-start | bytes 5734400 | tf_op jit(solution)/shard_map/all_gather | solution.py:100
  70.6 14.6 %collective-permute-start.3 = (bf16[2,448]{1,0:T(2,128)(2,1)S(1)}, bf16[2,448]{1,0:T(2,128)(2,1)S(1)}, u32[]{:S(2)}, u32[]{:S(2)}) collective-permute-start(bf16[2,448]{1,0:T(2,128)(2,1)S(1)} %pad_maximum_fusion.15), channel_id=1, source_target_pairs={{0,24},{1,25},{2,26},{3,27},{4,28},{5,29},{6,30},{7,31},{8,0},{9,1... | collective-permute-start | bytes 5384 | tf_op jit(solution)/shard_map/ppermute | solution.py:31
  86.1 3.7 collective-permute-start.4
  90.7 410.9 %copy-start.52 = (f32[1792]{0:T(1024)}, f32[1792]{0:T(1024)S(1)}, u32[]{:S(2)}) copy-start(f32[1792]{0:T(1024)S(1)} %get-tuple-element.250) | copy-start | bytes 21508
  90.8 591.2 %copy-start.55 = (f32[1792]{0:T(1024)}, f32[1792]{0:T(1024)S(1)}, u32[]{:S(2)}) copy-start(f32[1792]{0:T(1024)S(1)} %get-tuple-element.249) | copy-start | bytes 21508
  122.1 121.0 %all-gather.12.cloned.1.call-start = ((), (), s32[]{:S(2)}) async-start(), calls=%async_computation.12 | async-start | bytes 4128768 | tf_op jit(solution)/shard_map/all_gather | solution.py:67
  130.5 12.2 %copy-start.4 = (bf16[16,64,288]{2,1,0:T(8,128)(2,1)}, bf16[16,64,288]{2,1,0:T(8,128)(2,1)S(1)}, u32[]{:S(2)}) copy-start(bf16[16,64,288]{2,1,0:T(8,128)(2,1)S(1)} %broadcast_select_fusion.1) | copy-start | bytes 1769476
  196.6 95.5 %all-gather.14.cloned.1.call-start = ((), (), s32[]{:S(2)}) async-start(), calls=%async_computation.13 | async-start | bytes 2723840 | tf_op jit(solution)/shard_map/all_gather | solution.py:228
  198.3 128.8 %all-gather.22.cloned.1.call-start = ((), (), s32[]{:S(2)}) async-start(), calls=%async_computation.17 | async-start | bytes 4128768 | tf_op jit(solution)/shard_map/all_gather | solution.py:67
  335.4 9.7 %copy-start.105 = (bf16[1024,608]{0,1:T(8,128)(2,1)}, bf16[1024,608]{0,1:T(8,128)(2,1)S(1)}, u32[]{:S(2)}) copy-start(bf16[1024,608]{0,1:T(8,128)(2,1)S(1)} %get-tuple-element.273) | copy-start | bytes 3735556
  335.4 9.7 %copy-start.106 = (bf16[1024,608]{0,1:T(8,128)(2,1)}, bf16[1024,608]{0,1:T(8,128)(2,1)S(1)}, u32[]{:S(2)}) copy-start(bf16[1024,608]{0,1:T(8,128)(2,1)S(1)} %get-tuple-element.274) | copy-start | bytes 3735556
  345.1 48.2 %all-to-all-start.4 = ((bf16[8,128,1792]{2,1,0:T(8,128)(2,1)}), bf16[8,128,1792]{2,1,0:T(8,128)(2,1)}, u32[]{:S(2)}, u32[]{:S(2)}) async-start(bf16[8,128,1792]{2,1,0:T(8,128)(2,1)} %bitcast.359), calls=%async_computation.4 | async-start | bytes 7340032 | tf_op jit(solution)/shard_map/all_to_all | solution.py:72
  393.3 48.0 %all-to-all-start.3 = ((bf16[8,128,1792]{2,1,0:T(8,128)(2,1)}), bf16[8,128,1792]{2,1,0:T(8,128)(2,1)}, u32[]{:S(2)}, u32[]{:S(2)}) async-start(bf16[8,128,1792]{2,1,0:T(8,128)(2,1)} %bitcast.358), calls=%async_computation.3 | async-start | bytes 7340032 | tf_op jit(solution)/shard_map/all_to_all | solution.py:72
  441.3 51.8 %all-to-all-start.11 = ((bf16[4,152,1792]{2,1,0:T(8,128)(2,1)}), bf16[4,152,1792]{2,1,0:T(8,128)(2,1)}, u32[]{:S(2)}, u32[]{:S(2)}) async-start(bf16[4,152,1792]{2,1,0:T(8,128)(2,1)} %bitcast.361), calls=%async_computation.11 | async-start | bytes 4358144 | tf_op jit(solution)/shard_map/all_to_all | solution.py:116
  493.2 106.1 %all-to-all-start.9 = ((bf16[1,8,4,56,1216]{4,3,1,0,2:T(8,128)(2,1)}), bf16[1,8,4,56,1216]{4,3,1,0,2:T(8,128)(2,1)}, u32[]{:S(2)}, u32[]{:S(2)}) async-start(bf16[1,8,4,56,1216]{4,3,1,0,2:T(8,128)(2,1)} %copy.366), calls=%async_computation.9 | async-start | bytes 9175040 | tf_op jit(solution)/shard_map/all_to_all | solution.py:107
  498.1 133.2 %all-gather.16.cloned.1.call-start = ((), (), s32[]{:S(2)}) async-start(), calls=%async_computation.14 | async-start | bytes 4128768 | tf_op jit(solution)/shard_map/all_gather | solution.py:67
  501.6 10.0 %copy-start.93 = (f32[2,3,56]{2,0,1:T(2,128)S(1)}, f32[2,3,56]{2,0,1:T(2,128)}, u32[]{:S(2)}) copy-start(f32[2,3,56]{2,0,1:T(2,128)} %param.45) | copy-start | bytes 4036
  502.5 10.8 %copy-start.94 = (f32[128]{0:T(128)}, f32[128]{0:T(128)S(1)}, u32[]{:S(2)}) copy-start(f32[128]{0:T(128)S(1)} %broadcast_multiply_fusion.1) | copy-start | bytes 1540
  519.2 92.9 %copy-start.5 = (f32[152,1792]{1,0:T(8,128)}, f32[152,1792]{1,0:T(8,128)S(1)}, u32[]{:S(2)}) copy-start(f32[152,1792]{1,0:T(8,128)S(1)} %convert_reduce_fusion.4) | copy-start | bytes 3268612
  603.6 21.5 %all-to-all-start.10 = ((bf16[8,56,1216]{2,1,0:T(8,128)(2,1)}), bf16[8,56,1216]{2,1,0:T(8,128)(2,1)}, u32[]{:S(2)}, u32[]{:S(2)}) async-start(bf16[8,56,1216]{2,1,0:T(8,128)(2,1)} %reduce_sum.346), calls=%async_computation.10 | async-start | bytes 2293760 | tf_op jit(solution)/shard_map/all_to_all | solution.py:109
  626.7 9.0 copy-start.14
  631.3 7.3 copy-start.88
  668.3 10.1 %copy-start.65 = (f32[1,224]{1,0:T(1,128)S(1)}, f32[1,224]{1,0:T(1,128)}, u32[]{:S(2)}) copy-start(f32[1,224]{1,0:T(1,128)} %get-tuple-element.316) | copy-start | bytes 2692
  668.3 10.1 %copy-start.67 = (f32[1,224]{1,0:T(1,128)S(1)}, f32[1,224]{1,0:T(1,128)}, u32[]{:S(2)}) copy-start(f32[1,224]{1,0:T(1,128)} %get-tuple-element.317) | copy-start | bytes 2692
  690.4 34.5 %all-to-all-start.6 = ((bf16[1,8,4,56,288]{4,3,1,0,2:T(8,128)(2,1)}), bf16[1,8,4,56,288]{4,3,1,0,2:T(8,128)(2,1)}, u32[]{:S(2)}, u32[]{:S(2)}) async-start(bf16[1,8,4,56,288]{4,3,1,0,2:T(8,128)(2,1)} %copy.358), calls=%async_computation.6 | async-start | bytes 2752512 | tf_op jit(solution)/shard_map/all_to_all | solution.py:107
  703.9 6.9 copy-start.26
  703.9 6.9 copy-start.103
  724.9 26.0 %all-to-all-start.8 = ((bf16[4,56,1792]{2,1,0:T(8,128)(2,1)}), bf16[4,56,1792]{2,1,0:T(8,128)(2,1)}, u32[]{:S(2)}, u32[]{:S(2)}) async-start(bf16[4,56,1792]{2,1,0:T(8,128)(2,1)} %bitcast.368), calls=%async_computation.8 | async-start | bytes 1605632 | tf_op jit(solution)/shard_map/all_to_all | solution.py:116
  733.2 23.0 %copy-start.39 = (bf16[1792,288]{0,1:T(8,128)(2,1)S(1)}, bf16[1792,288]{0,1:T(8,128)(2,1)}, u32[]{:S(2)}) copy-start(bf16[1792,288]{0,1:T(8,128)(2,1)} %copy-done.38) | copy-start | bytes 3096580
  733.2 23.0 %copy-start.41 = (bf16[16,64,288]{2,1,0:T(8,128)(2,1)S(1)}, bf16[16,64,288]{2,1,0:T(8,128)(2,1)}, u32[]{:S(2)}) copy-start(bf16[16,64,288]{2,1,0:T(8,128)(2,1)} %copy-done.40) | copy-start | bytes 1769476
  750.9 13.0 %all-to-all-start.7 = ((bf16[8,56,288]{2,1,0:T(8,128)(2,1)}), bf16[8,56,288]{2,1,0:T(8,128)(2,1)S(1)}, u32[]{:S(2)}, u32[]{:S(2)}) async-start(bf16[8,56,288]{2,1,0:T(8,128)(2,1)} %reduce_sum.341), calls=%async_computation.7 | async-start | bytes 688128 | tf_op jit(solution)/shard_map/all_to_all | solution.py:109
  763.9 7.9 copy-start.28
  763.9 48.1 %all-to-all-start.5 = ((bf16[8,128,1792]{2,1,0:T(8,128)(2,1)}), bf16[8,128,1792]{2,1,0:T(8,128)(2,1)}, u32[]{:S(2)}, u32[]{:S(2)}) async-start(bf16[8,128,1792]{2,1,0:T(8,128)(2,1)} %bitcast.357), calls=%async_computation.5 | async-start | bytes 7340032 | tf_op jit(solution)/shard_map/all_to_all | solution.py:72
  779.1 35.6 %copy-start.56 = (f32[1792]{0:T(1024)S(1)}, f32[1792]{0:T(1024)}, u32[]{:S(2)}) copy-start(f32[1792]{0:T(1024)} %copy-done.55) | copy-start | bytes 21508
  779.1 35.6 %copy-start.96 = (f32[128]{0:T(128)S(1)}, f32[128]{0:T(128)}, u32[]{:S(2)}) copy-start(f32[128]{0:T(128)} %add_rsqrt_fusion.1) | copy-start | bytes 1540
  779.1 35.9 %copy-start.60 = (f32[1,1792]{1,0:T(1,128)S(1)}, f32[1,1792]{1,0:T(1,128)}, u32[]{:S(2)}) copy-start(f32[1,1792]{1,0:T(1,128)} %stack.133) | copy-start | bytes 21508
  779.1 78.2 %copy-start.91 = (f32[2,56]{1,0:T(2,128)S(1)}, f32[2,56]{1,0:T(2,128)}, u32[]{:S(2)}) copy-start(f32[2,56]{1,0:T(2,128)} %param.47) | copy-start | bytes 1348
  779.1 78.2 %copy-start.92 = (f32[2,56]{1,0:T(2,128)S(1)}, f32[2,56]{1,0:T(2,128)}, u32[]{:S(2)}) copy-start(f32[2,56]{1,0:T(2,128)} %param.43) | copy-start | bytes 1348
  779.1 83.9 %copy-start.101 = (f32[7]{0:T(128)S(1)}, f32[7]{0:T(128)}, u32[]{:S(2)}) copy-start(f32[7]{0:T(128)} %stack.155) | copy-start | bytes 88
  779.1 132.9 %copy-start.2 = (f32[128,1792]{1,0:T(8,128)S(1)}, f32[128,1792]{1,0:T(8,128)}, u32[]{:S(2)}) copy-start(f32[128,1792]{1,0:T(8,128)} %copy-done.1) | copy-start | bytes 2752516
  779.1 132.9 %copy-start.53 = (f32[1792]{0:T(1024)S(1)}, f32[1792]{0:T(1024)}, u32[]{:S(2)}) copy-start(f32[1792]{0:T(1024)} %copy-done.52) | copy-start | bytes 21508
  779.1 132.9 %copy-start.79 = (f32[128]{0:T(128)S(1)}, f32[128]{0:T(128)}, u32[]{:S(2)}) copy-start(f32[128]{0:T(128)} %copy-done.77) | copy-start | bytes 1540
  779.1 132.9 %copy-start.95 = (f32[128]{0:T(128)S(1)}, f32[128]{0:T(128)}, u32[]{:S(2)}) copy-start(f32[128]{0:T(128)} %copy-done.94) | copy-start | bytes 1540
  902.1 13.1 %copy-start.57 = (f32[2,7]{1,0:T(2,128)}, f32[2,7]{1,0:T(2,128)S(1)}, u32[]{:S(2)}) copy-start(f32[2,7]{1,0:T(2,128)S(1)} %sqrt.31) | copy-start | bytes 172
  912.1 6.2 copy-start.34
  912.1 6.2 copy-start.35
  912.1 7.5 copy-start.10
  (65 other events, 187.2 us)
Sparse Core Ops, SparseCore 0:
  9.9 39.1 all-gather.17
  122.2 85.5 all-gather.19
  210.2 32.8 all-gather.11
  245.1 46.9 all-gather.13
  293.9 33.1 all-gather.21
  503.8 36.9 all-gather.15
